TPU v7x, 32 devices: a whole 2x2x4 slice. The times are simulated.
32 devices in a mesh: shard: 16 (over z, y, core), model: 2 (over x).
Axes of the slice: x: 2, y: 2, z: 4, core: 2. Of those that a mesh axis runs over, the one named last changes fastest.
Arguments:
- gradients: float32 [128, 128, 4096], P(None, 'shard', 'model'), may hold values from -6 to 6
- momentum: float32 [128, 128, 4096], P(None, 'shard', 'model'), may hold values from -6 to 6
- weights: float32 [128, 128, 4096], P(None, 'shard', 'model'), may hold values from -0.1875 to 0.1875
Outputs:
- new_weights: float32 [128, 128, 4096], P(None, 'shard', 'model')
- new_momentum: float32 [128, 128, 4096], P(None, 'shard', 'model')
All inputs are finite; a program needn't handle non-finite values.
Results may differ from a plain program's by a relative error of at most 0.00012.
Values sent between devices are 32-bit elements; how exact they have to be, the bound alone decides.
A program may use at most 128 MiB of HBM per device.

v0:
```python
import jax
import jax.numpy as jnp
from jax import lax
from jax.sharding import PartitionSpec as P

ITERS = 4
hold_rate = 0.9
learn_rate = 0.8


def local(gradients, momentum, weights):
    new_momentum = hold_rate * momentum + gradients
    direction = hold_rate * new_momentum + gradients
    moved = lax.all_to_all(direction, "shard", split_axis=0, concat_axis=1, tiled=True)
    total = lax.psum(jnp.sum(moved * moved, axis=(1, 2), keepdims=True), "model")
    iterate = moved * lax.rsqrt(total + 1e-06)
    for step in range(ITERS):
        gram = lax.psum(
            jnp.einsum("mik,mjk->mij", iterate, iterate, precision=lax.Precision.HIGHEST), "model"
        )
        mixed = -4.775 * gram + 2.0315 * jnp.einsum(
            "mij,mjk->mik", gram, gram, precision=lax.Precision.HIGHEST
        )
        iterate = 3.4445 * iterate + jnp.einsum(
            "mij,mjk->mik", mixed, iterate, precision=lax.Precision.HIGHEST
        )
    back = lax.all_to_all(iterate, "shard", split_axis=1, concat_axis=0, tiled=True)
    new_weights = weights - learn_rate * back
    return (new_weights, new_momentum)


def solution(mesh):
    return jax.shard_map(
        local,
        mesh=mesh,
        in_specs=(P(None, "shard", "model"), P(None, "shard", "model"), P(None, "shard", "model")),
        out_specs=(P(None, "shard", "model"), P(None, "shard", "model")),
        check_vma=False,
    )
```

profile of v0, /device:TPU:1, one launch (start us, length us, event | category | flops | bytes accessed | tf_op | source)
XLA Modules:
  0.0 666.5 jit_solution(225198048523611833)
XLA Ops:
  7.2 9.3 %multiply_add_fusion.4 = (f32[128,8,2048]{2,1,0:T(8,128)S(1)}, f32[128,8,2048]{2,1,0:T(8,128)}) fusion(f32[128,8,2048]{2,1,0:T(8,128)} %param.3, f32[128,8,2048]{2,1,0:T(8,128)} %param.4), kind=kLoop, calls=%fused_computation.8 | loop fusion | flops 8388608 | bytes 33554432 | tf_op jit(solution)/shard_map/add | solution.py:13
  16.5 189.7 %all_to_all.27 = f32[128,8,2048]{2,1,0:T(8,128)S(1)} all-to-all(f32[128,8,2048]{2,1,0:T(8,128)S(1)} %get-tuple-element.2), channel_id=1, replica_groups=mesh['shard'=16,'model'=2] {'shard'}, dimensions={0} | all-to-all | bytes 16777216 | tf_op jit(solution)/shard_map/all_to_all | solution.py:14
  206.2 3.4 copy-done
  210.3 4.1 psum.35
  214.4 12.9 %fusion.2 = f32[8,128,128]{2,1,0:T(8,128)} fusion(f32[16,8,8,2048]{3,2,1,0:T(8,128)} %bitcast.44, f32[8]{0:T(128)S(1)} %rsqrt_bitcast_fusion), kind=kOutput, calls=%fused_computation.11 | convolution fusion | flops 3223322624 | bytes 8912928 | tf_op jit(solution)/shard_map/mik,mjk->mij/dot_general | solution.py:19
  227.4 29.3 %all-reduce.5.cloned.1.call-done = f32[8,128,128]{2,1,0:T(8,128)} async-done(((f32[8,128,128]{2,1,0:T(8,128)}), f32[8,128,128]{2,1,0:T(8,128)}) %all-reduce.5.cloned.1.call-update) | async-done | bytes 524304 | tf_op jit(solution)/shard_map/psum | solution.py:18
  258.8 11.7 %multiply_add_fusion.3 = f32[8,128,2048]{2,1,0:T(8,128)S(1)} fusion(f32[16,8,8,2048]{3,2,1,0:T(8,128)} %bitcast.45, f32[8,128,128]{2,1,0:T(8,128)S(1)} %fusion.8, f32[8]{0:T(128)S(1)} %rsqrt_bitcast_fusion), kind=kOutput, calls=%fused_computation.7 | convolution fusion | flops 3229614080 | bytes 17301536 | tf_op jit(solution)/shard_map/mij,mjk->mik/dot_general | solution.py:24
  270.5 3.4 copy-done.1
  273.9 8.5 %fusion.9 = f32[8,128,128]{2,1,0:T(8,128)} fusion(f32[8,128,2048]{2,1,0:T(8,128)S(1)} %multiply_add_fusion.3), kind=kOutput, calls=%fused_computation.24 | convolution fusion | flops 3221225472 | bytes 8912896 | tf_op jit(solution)/shard_map/mik,mjk->mij/dot_general | solution.py:19
  282.5 28.8 %all-reduce.7.cloned.1.call-done = f32[8,128,128]{2,1,0:T(8,128)} async-done(((f32[8,128,128]{2,1,0:T(8,128)}), f32[8,128,128]{2,1,0:T(8,128)}) %all-reduce.7.cloned.1.call-update) | async-done | bytes 524304 | tf_op jit(solution)/shard_map/psum | solution.py:18
  311.3 2.1 fusion.7
  313.3 14.3 %multiply_add_fusion.2 = f32[8,128,2048]{2,1,0:T(8,128)S(1)} fusion(f32[8,128,2048]{2,1,0:T(8,128)} %copy-done.1, f32[8,128,128]{2,1,0:T(8,128)S(1)} %fusion.7), kind=kOutput, calls=%fused_computation.6 | convolution fusion | flops 3225419776 | bytes 17301504 | tf_op jit(solution)/shard_map/mij,mjk->mik/dot_general | solution.py:24
  327.7 3.4 copy-done.2
  331.1 8.5 %fusion.10 = f32[8,128,128]{2,1,0:T(8,128)} fusion(f32[8,128,2048]{2,1,0:T(8,128)S(1)} %multiply_add_fusion.2), kind=kOutput, calls=%fused_computation.25 | convolution fusion | flops 3221225472 | bytes 8912896 | tf_op jit(solution)/shard_map/mik,mjk->mij/dot_general | solution.py:19
  339.7 28.8 %all-reduce.9.cloned.1.call-done = f32[8,128,128]{2,1,0:T(8,128)} async-done(((f32[8,128,128]{2,1,0:T(8,128)}), f32[8,128,128]{2,1,0:T(8,128)}) %all-reduce.9.cloned.1.call-update) | async-done | bytes 524304 | tf_op jit(solution)/shard_map/psum | solution.py:18
  370.5 14.1 %multiply_add_fusion.1 = f32[8,128,2048]{2,1,0:T(8,128)S(1)} fusion(f32[8,128,2048]{2,1,0:T(8,128)} %copy-done.2, f32[8,128,128]{2,1,0:T(8,128)S(1)} %fusion.6), kind=kOutput, calls=%fused_computation.5 | convolution fusion | flops 3225419776 | bytes 17301504 | tf_op jit(solution)/shard_map/mij,mjk->mik/dot_general | solution.py:24
  384.7 3.4 copy-done.3
  388.1 8.5 %fusion.11 = f32[8,128,128]{2,1,0:T(8,128)} fusion(f32[8,128,2048]{2,1,0:T(8,128)S(1)} %multiply_add_fusion.1), kind=kOutput, calls=%fused_computation.26 | convolution fusion | flops 3221225472 | bytes 8912896 | tf_op jit(solution)/shard_map/mik,mjk->mij/dot_general | solution.py:19
  396.6 28.8 %all-reduce.11.cloned.1.call-done = f32[8,128,128]{2,1,0:T(8,128)} async-done(((f32[8,128,128]{2,1,0:T(8,128)}), f32[8,128,128]{2,1,0:T(8,128)}) %all-reduce.11.cloned.1.call-update) | async-done | bytes 524304 | tf_op jit(solution)/shard_map/psum | solution.py:18
  427.5 14.9 %multiply_add_fusion = f32[8,128,2048]{2,1,0:T(8,128)S(1)} fusion(f32[8,128,2048]{2,1,0:T(8,128)} %copy-done.3, f32[8,128,128]{2,1,0:T(8,128)S(1)} %fusion.5), kind=kOutput, calls=%fused_computation.4 | convolution fusion | flops 3225419776 | bytes 17301504 | tf_op jit(solution)/shard_map/mij,mjk->mik/dot_general | solution.py:24
  442.4 4.9 copy.8
  447.2 188.9 %all_to_all.28 = f32[8,128,2048]{2,0,1:T(8,128)S(1)} all-to-all(f32[8,128,2048]{2,0,1:T(8,128)S(1)} %copy.8), channel_id=1, replica_groups=mesh['shard'=16,'model'=2] {'shard'}, dimensions={1} | all-to-all | bytes 16777216 | tf_op jit(solution)/shard_map/all_to_all | solution.py:27
  638.0 9.7 %copy.9 = f32[16,8,8,2048]{3,2,1,0:T(8,128)} copy(f32[16,8,8,2048]{3,1,2,0:T(8,128)S(1)} %bitcast.46) | data formatting | bytes 16777216 | tf_op jit(solution)/shard_map/mul | solution.py:28
  647.7 11.9 %bitcast_subtract_fusion = f32[128,8,2048]{2,1,0:T(8,128)} fusion(f32[128,8,2048]{2,1,0:T(8,128)} %param.5, f32[16,8,8,2048]{3,2,1,0:T(8,128)} %copy.9), kind=kLoop, calls=%fused_computation.1 | loop fusion | flops 2097152 | bytes 25165824 | tf_op jit(solution)/shard_map/sub | solution.py:28
  (18 shorter events, 9.1 us)
Async XLA Ops:
  7.2 249.5 %all-reduce.5.cloned.1.call-start = ((), (), s32[]{:S(2)}) async-start(), calls=%async_computation.2 | async-start | bytes 1048576 | tf_op jit(solution)/shard_map/psum | solution.py:18
  206.2 3.4 copy-start
  227.3 83.9 %all-reduce.7.cloned.1.call-start = ((), (), s32[]{:S(2)}) async-start(), calls=%async_computation.3 | async-start | bytes 1048576 | tf_op jit(solution)/shard_map/psum | solution.py:18
  270.5 3.4 copy-start.1
  282.4 86.0 %all-reduce.9.cloned.1.call-start = ((), (), s32[]{:S(2)}) async-start(), calls=%async_computation.4 | async-start | bytes 1048576 | tf_op jit(solution)/shard_map/psum | solution.py:18
  327.7 3.4 copy-start.2
  339.6 85.8 %all-reduce.11.cloned.1.call-start = ((), (), s32[]{:S(2)}) async-start(), calls=%async_computation.5 | async-start | bytes 1048576 | tf_op jit(solution)/shard_map/psum | solution.py:18
  384.7 3.4 copy-start.3
Sparse Core Ops, SparseCore 0:
  227.5 29.1 all-reduce.4
  282.6 28.6 all-reduce.6
  339.8 28.6 all-reduce.8
  396.7 28.6 all-reduce.10
where the time goes:
time: 675 us; the launch traced here: 667 us
  blocking collectives  383 us (57%)
  waiting for transfers between devices  116 us (17%)
  matrix products  102 us (15%)
  local copies, waits for them, and re-layouts  28.1 us (4%)
  other arithmetic  23.8 us (4%)
  between operations  14.3 us (2%)
    all_to_all x1, blocking collectives, local(): lax.all_to_all(direction, 'shard', split_axis=0, concat_axis=1, tiled=True)  190 us
    all_to_all x1, blocking collectives, local(): lax.all_to_all(iterate, 'shard', split_axis=1, concat_axis=0, tiled=True)  189 us
    psum x4, waiting for transfers between devices, local(): lax.psum(jnp.einsum('mik,mjk->mij', iterate, iterate, precision=lax.Preci...  116 us
    dot_general x4, matrix products, local(): jnp.einsum('mij,mjk->mik', mixed, iterate, precision=lax.Precision.HIGHEST)  55 us
    dot_general x4, matrix products, local(): jnp.einsum('mik,mjk->mij', iterate, iterate, precision=lax.Precision.HIGH...  38.5 us
    unnamed x8, local copies, waits for them, and re-layouts  13.6 us
  transfers between devices with their start and end apart: 4, of which 4 were waited for; matrix products, arithmetic and copies ran while one was open for 0% of the time, Pallas kernels for 0%

commit v1 on v0

--- a/solution.py
+++ b/solution.py
@@ -11,7 +11,12 @@
 def local(gradients, momentum, weights):
     new_momentum = hold_rate * momentum + gradients
     direction = hold_rate * new_momentum + gradients
-    moved = lax.all_to_all(direction, "shard", split_axis=0, concat_axis=1, tiled=True)
+    moved = jnp.concatenate(
+        lax.all_to_all(
+            jnp.stack(jnp.split(direction, lax.axis_size("shard"), axis=0)), "shard", 0, 0
+        ),
+        axis=1,
+    )
     total = lax.psum(jnp.sum(moved * moved, axis=(1, 2), keepdims=True), "model")
     iterate = moved * lax.rsqrt(total + 1e-06)
     for step in range(ITERS):

time: 675 us -> 673 us (level)
    unnamed x8 -> x23, local copies, waits for them, and re-layouts: 13.6 us -> 14.1 us
where the time goes in v1:
time: 673 us; the launch traced here: 667 us
  blocking collectives  383 us (57%)
  waiting for transfers between devices  115 us (17%)
  matrix products  102 us (15%)
  local copies, waits for them, and re-layouts  28.7 us (4%)
  other arithmetic  23.8 us (4%)
  between operations  14.4 us (2%)
    all_to_all x1, blocking collectives, local(): lax.all_to_all(jnp.stack(jnp.split(direction, lax.axis_size('shard'), axi...  190 us
    all_to_all x1, blocking collectives, local(): lax.all_to_all(iterate, 'shard', split_axis=1, concat_axis=0, tiled=True)  189 us
    psum x4, waiting for transfers between devices, local(): lax.psum(jnp.einsum('mik,mjk->mij', iterate, iterate, precision=lax.Preci...  115 us
    dot_general x4, matrix products, local(): jnp.einsum('mij,mjk->mik', mixed, iterate, precision=lax.Precision.HIGHEST)  55.1 us
    dot_general x4, matrix products, local(): jnp.einsum('mik,mjk->mij', iterate, iterate, precision=lax.Precision.HIGH...  38.5 us
    unnamed x23, local copies, waits for them, and re-layouts  14.1 us
  transfers between devices with their start and end apart: 4, of which 4 were waited for; matrix products, arithmetic and copies ran while one was open for 0% of the time, Pallas kernels for 0%

profile of v1, /device:TPU:1, one launch (start us, length us, event | category | flops | bytes accessed | tf_op | source)
XLA Modules:
  0.0 667.3 jit_solution(2204244246811271638)
XLA Ops:
  7.2 9.3 %multiply_add_fusion.4 = (f32[128,8,2048]{2,1,0:T(8,128)S(1)}, f32[128,8,2048]{2,1,0:T(8,128)}) fusion(f32[128,8,2048]{2,1,0:T(8,128)} %param.3, f32[128,8,2048]{2,1,0:T(8,128)} %param.4), kind=kLoop, calls=%fused_computation.7 | loop fusion | flops 8388608 | bytes 33554432 | tf_op jit(solution)/shard_map/add | solution.py:13
  17.2 189.7 %all_to_all.14 = f32[16,8,8,2048]{3,2,1,0:T(8,128)S(1)} all-to-all(f32[16,8,8,2048]{3,2,1,0:T(8,128)S(1)} %fusion.8), channel_id=1, replica_groups=mesh['shard'=16,'model'=2] {'shard'}, dimensions={0} | all-to-all | bytes 16777216 | tf_op jit(solution)/shard_map/all_to_all | solution.py:15
  206.9 3.4 copy-done
  211.1 4.1 psum.35
  215.1 12.9 %fusion.1 = f32[8,128,128]{2,1,0:T(8,128)} fusion(f32[8]{0:T(128)S(1)} %rsqrt_bitcast_fusion, f32[16,8,8,2048]{3,2,1,0:T(8,128)} %copy-done), kind=kOutput, calls=%fused_computation.10 | convolution fusion | flops 3223322624 | bytes 8912928 | tf_op jit(solution)/shard_map/mik,mjk->mij/dot_general | solution.py:24
  228.3 29.1 %all-reduce.5.cloned.1.call-done = f32[8,128,128]{2,1,0:T(8,128)} async-done(((f32[8,128,128]{2,1,0:T(8,128)}), f32[8,128,128]{2,1,0:T(8,128)}) %all-reduce.5.cloned.1.call-update) | async-done | bytes 524304 | tf_op jit(solution)/shard_map/psum | solution.py:23
  259.5 11.7 %multiply_add_fusion.3 = f32[8,128,2048]{2,1,0:T(8,128)S(1)} fusion(f32[8,128,128]{2,1,0:T(8,128)S(1)} %fusion.7, f32[8]{0:T(128)S(1)} %rsqrt_bitcast_fusion, f32[16,8,8,2048]{3,2,1,0:T(8,128)} %copy-done), kind=kOutput, calls=%fused_computation.5 | convolution fusion | flops 3229614080 | bytes 17301536 | tf_op jit(solution)/shard_map/mij,mjk->mik/dot_general | solution.py:29
  271.3 3.4 copy-done.1
  274.7 8.5 %fusion.24 = f32[8,128,128]{2,1,0:T(8,128)} fusion(f32[8,128,2048]{2,1,0:T(8,128)S(1)} %multiply_add_fusion.3), kind=kOutput, calls=%fused_computation.55 | convolution fusion | flops 3221225472 | bytes 8912896 | tf_op jit(solution)/shard_map/mik,mjk->mij/dot_general | solution.py:24
  283.3 28.8 %all-reduce.7.cloned.1.call-done = f32[8,128,128]{2,1,0:T(8,128)} async-done(((f32[8,128,128]{2,1,0:T(8,128)}), f32[8,128,128]{2,1,0:T(8,128)}) %all-reduce.7.cloned.1.call-update) | async-done | bytes 524304 | tf_op jit(solution)/shard_map/psum | solution.py:23
  312.0 2.1 fusion.6
  314.1 14.4 %multiply_add_fusion.2 = f32[8,128,2048]{2,1,0:T(8,128)S(1)} fusion(f32[8,128,2048]{2,1,0:T(8,128)} %copy-done.1, f32[8,128,128]{2,1,0:T(8,128)S(1)} %fusion.6), kind=kOutput, calls=%fused_computation.4 | convolution fusion | flops 3225419776 | bytes 17301504 | tf_op jit(solution)/shard_map/mij,mjk->mik/dot_general | solution.py:29
  328.5 3.4 copy-done.2
  331.9 8.5 %fusion.25 = f32[8,128,128]{2,1,0:T(8,128)} fusion(f32[8,128,2048]{2,1,0:T(8,128)S(1)} %multiply_add_fusion.2), kind=kOutput, calls=%fused_computation.56 | convolution fusion | flops 3221225472 | bytes 8912896 | tf_op jit(solution)/shard_map/mik,mjk->mij/dot_general | solution.py:24
  340.5 28.7 %all-reduce.9.cloned.1.call-done = f32[8,128,128]{2,1,0:T(8,128)} async-done(((f32[8,128,128]{2,1,0:T(8,128)}), f32[8,128,128]{2,1,0:T(8,128)}) %all-reduce.9.cloned.1.call-update) | async-done | bytes 524304 | tf_op jit(solution)/shard_map/psum | solution.py:23
  371.3 14.1 %multiply_add_fusion.1 = f32[8,128,2048]{2,1,0:T(8,128)S(1)} fusion(f32[8,128,2048]{2,1,0:T(8,128)} %copy-done.2, f32[8,128,128]{2,1,0:T(8,128)S(1)} %fusion.5), kind=kOutput, calls=%fused_computation.3 | convolution fusion | flops 3225419776 | bytes 17301504 | tf_op jit(solution)/shard_map/mij,mjk->mik/dot_general | solution.py:29
  385.5 3.4 copy-done.3
  388.9 8.5 %fusion.26 = f32[8,128,128]{2,1,0:T(8,128)} fusion(f32[8,128,2048]{2,1,0:T(8,128)S(1)} %multiply_add_fusion.1), kind=kOutput, calls=%fused_computation.57 | convolution fusion | flops 3221225472 | bytes 8912896 | tf_op jit(solution)/shard_map/mik,mjk->mij/dot_general | solution.py:24
  397.4 28.8 %all-reduce.11.cloned.1.call-done = f32[8,128,128]{2,1,0:T(8,128)} async-done(((f32[8,128,128]{2,1,0:T(8,128)}), f32[8,128,128]{2,1,0:T(8,128)}) %all-reduce.11.cloned.1.call-update) | async-done | bytes 524304 | tf_op jit(solution)/shard_map/psum | solution.py:23
  428.3 14.9 %multiply_add_fusion = f32[8,128,2048]{2,1,0:T(8,128)S(1)} fusion(f32[8,128,2048]{2,1,0:T(8,128)} %copy-done.3, f32[8,128,128]{2,1,0:T(8,128)S(1)} %fusion.4), kind=kOutput, calls=%fused_computation.2 | convolution fusion | flops 3225419776 | bytes 17301504 | tf_op jit(solution)/shard_map/mij,mjk->mik/dot_general | solution.py:29
  443.1 4.9 copy.8
  448.0 188.9 %all_to_all.15 = f32[8,128,2048]{2,0,1:T(8,128)S(1)} all-to-all(f32[8,128,2048]{2,0,1:T(8,128)S(1)} %copy.8), channel_id=1, replica_groups=mesh['shard'=16,'model'=2] {'shard'}, dimensions={1} | all-to-all | bytes 16777216 | tf_op jit(solution)/shard_map/all_to_all | solution.py:32
  638.8 9.7 %copy.9 = f32[16,8,8,2048]{3,2,1,0:T(8,128)} copy(f32[16,8,8,2048]{3,1,2,0:T(8,128)S(1)} %bitcast.110) | data formatting | bytes 16777216 | tf_op jit(solution)/shard_map/mul | solution.py:33
  648.5 11.9 %bitcast_subtract_fusion = f32[128,8,2048]{2,1,0:T(8,128)} fusion(f32[128,8,2048]{2,1,0:T(8,128)} %param.5, f32[16,8,8,2048]{3,2,1,0:T(8,128)} %copy.9), kind=kLoop, calls=%fused_computation | loop fusion | flops 2097152 | bytes 25165824 | tf_op jit(solution)/shard_map/sub | solution.py:33
  (34 shorter events, 9.9 us)
Async XLA Ops:
  7.2 250.3 %all-reduce.5.cloned.1.call-start = ((), (), s32[]{:S(2)}) async-start(), calls=%async_computation.2 | async-start | bytes 1048576 | tf_op jit(solution)/shard_map/psum | solution.py:23
  206.9 3.4 copy-start
  228.1 84.0 %all-reduce.7.cloned.1.call-start = ((), (), s32[]{:S(2)}) async-start(), calls=%async_computation.3 | async-start | bytes 1048576 | tf_op jit(solution)/shard_map/psum | solution.py:23
  271.3 3.4 copy-start.1
  283.2 86.0 %all-reduce.9.cloned.1.call-start = ((), (), s32[]{:S(2)}) async-start(), calls=%async_computation.4 | async-start | bytes 1048576 | tf_op jit(solution)/shard_map/psum | solution.py:23
  328.5 3.4 copy-start.2
  340.5 85.7 %all-reduce.11.cloned.1.call-start = ((), (), s32[]{:S(2)}) async-start(), calls=%async_computation.5 | async-start | bytes 1048576 | tf_op jit(solution)/shard_map/psum | solution.py:23
  385.4 3.4 copy-start.3
Sparse Core Ops, SparseCore 0:
  228.2 29.1 all-reduce.4
  283.3 28.6 all-reduce.6
  340.6 28.6 all-reduce.8
  397.5 28.6 all-reduce.10

commit v2 on v0

--- a/solution.py
+++ b/solution.py
@@ -15,8 +15,12 @@
     total = lax.psum(jnp.sum(moved * moved, axis=(1, 2), keepdims=True), "model")
     iterate = moved * lax.rsqrt(total + 1e-06)
     for step in range(ITERS):
-        gram = lax.psum(
-            jnp.einsum("mik,mjk->mij", iterate, iterate, precision=lax.Precision.HIGHEST), "model"
+        gram = jnp.sum(
+            lax.all_gather(
+                jnp.einsum("mik,mjk->mij", iterate, iterate, precision=lax.Precision.HIGHEST),
+                "model",
+            ),
+            axis=0,
         )
         mixed = -4.775 * gram + 2.0315 * jnp.einsum(
             "mij,mjk->mik", gram, gram, precision=lax.Precision.HIGHEST

time: 675 us -> 645 us (0.956)
  waiting for transfers between devices: 116 us -> 86.2 us
    psum x4 -> x0, waiting for transfers between devices: 116 us -> none  [local(): lax.psum(jnp.einsum('mik,mjk->mij', iterate, iterate, precision=lax.Preci...]
    all_gather x0 -> x4, waiting for transfers between devices: none -> 86.2 us  [local(): lax.all_gather(jnp.einsum('mik,mjk->mij', iterate, iterate, precision=lax...]
where the time goes in v2:
time: 645 us; the launch traced here: 637 us
  blocking collectives  383 us (59%)
  matrix products  96.2 us (15%)
  waiting for transfers between devices  86.2 us (13%)
  other arithmetic  29.1 us (5%)
  local copies, waits for them, and re-layouts  28.1 us (4%)
  between operations  14.3 us (2%)
    all_to_all x1, blocking collectives, local(): lax.all_to_all(direction, 'shard', split_axis=0, concat_axis=1, tiled=True)  190 us
    all_to_all x1, blocking collectives, local(): lax.all_to_all(iterate, 'shard', split_axis=1, concat_axis=0, tiled=True)  189 us
    all_gather x4, waiting for transfers between devices, local(): lax.all_gather(jnp.einsum('mik,mjk->mij', iterate, iterate, precision=lax...  86.2 us
    dot_general x4, matrix products, local(): jnp.einsum('mij,mjk->mik', mixed, iterate, precision=lax.Precision.HIGHEST)  55 us
    dot_general x4, matrix products, local(): jnp.einsum('mik,mjk->mij', iterate, iterate, precision=lax.Precision.HIGH...  38.5 us
    unnamed x8, local copies, waits for them, and re-layouts  13.6 us
  transfers between devices with their start and end apart: 4, of which 4 were waited for; matrix products, arithmetic and copies ran while one was open for 0% of the time, Pallas kernels for 0%

profile of v2, /device:TPU:1, one launch (start us, length us, event | category | flops | bytes accessed | tf_op | source)
XLA Modules:
  0.0 636.8 jit_solution(3586302549167066661)
XLA Ops:
  7.2 9.3 %multiply_add_fusion.4 = (f32[128,8,2048]{2,1,0:T(8,128)S(1)}, f32[128,8,2048]{2,1,0:T(8,128)}) fusion(f32[128,8,2048]{2,1,0:T(8,128)} %param.3, f32[128,8,2048]{2,1,0:T(8,128)} %param.4), kind=kLoop, calls=%fused_computation.8 | loop fusion | flops 8388608 | bytes 33554432 | tf_op jit(solution)/shard_map/add | solution.py:13
  16.5 189.7 %all_to_all.27 = f32[128,8,2048]{2,1,0:T(8,128)S(1)} all-to-all(f32[128,8,2048]{2,1,0:T(8,128)S(1)} %get-tuple-element.2), channel_id=1, replica_groups=mesh['shard'=16,'model'=2] {'shard'}, dimensions={0} | all-to-all | bytes 16777216 | tf_op jit(solution)/shard_map/all_to_all | solution.py:14
  206.2 3.4 copy-done
  210.3 4.1 psum.7
  214.4 12.9 %fusion.2 = f32[8,128,128]{2,1,0:T(8,128)} fusion(f32[16,8,8,2048]{3,2,1,0:T(8,128)} %bitcast.48, f32[8]{0:T(128)S(1)} %rsqrt_bitcast_fusion), kind=kOutput, calls=%fused_computation.11 | convolution fusion | flops 3223322624 | bytes 8912928 | tf_op jit(solution)/shard_map/mik,mjk->mij/dot_general | solution.py:20
  227.4 21.9 %all-gather.9.cloned.1.call-done = f32[16,128,128]{2,1,0:T(8,128)} async-done(((f32[8,128,128]{2,1,0:T(8,128)}), f32[16,128,128]{2,1,0:T(8,128)}) %all-gather.9.cloned.1.call-update) | async-done | bytes 1048592 | tf_op jit(solution)/shard_map/all_gather | solution.py:19
  251.4 11.7 %multiply_add_fusion.3 = f32[8,128,2048]{2,1,0:T(8,128)S(1)} fusion(f32[16,8,8,2048]{3,2,1,0:T(8,128)} %bitcast.49, f32[8,128,128]{2,1,0:T(8,128)S(1)} %fusion.8, f32[8]{0:T(128)S(1)} %rsqrt_bitcast_fusion), kind=kOutput, calls=%fused_computation.7 | convolution fusion | flops 3229614080 | bytes 17301536 | tf_op jit(solution)/shard_map/mij,mjk->mik/dot_general | solution.py:28
  263.1 3.4 copy-done.1
  266.5 8.5 %fusion.9 = f32[8,128,128]{2,1,0:T(8,128)} fusion(f32[8,128,2048]{2,1,0:T(8,128)S(1)} %multiply_add_fusion.3), kind=kOutput, calls=%fused_computation.24 | convolution fusion | flops 3221225472 | bytes 8912896 | tf_op jit(solution)/shard_map/mik,mjk->mij/dot_general | solution.py:20
  275.1 21.4 %all-gather.11.cloned.1.call-done = f32[16,128,128]{2,1,0:T(8,128)} async-done(((f32[8,128,128]{2,1,0:T(8,128)}), f32[16,128,128]{2,1,0:T(8,128)}) %all-gather.11.cloned.1.call-update) | async-done | bytes 1048592 | tf_op jit(solution)/shard_map/all_gather | solution.py:19
  298.5 14.3 %multiply_add_fusion.2 = f32[8,128,2048]{2,1,0:T(8,128)S(1)} fusion(f32[8,128,2048]{2,1,0:T(8,128)} %copy-done.1, f32[8,128,128]{2,1,0:T(8,128)S(1)} %fusion.7), kind=kOutput, calls=%fused_computation.6 | convolution fusion | flops 3225419776 | bytes 17301504 | tf_op jit(solution)/shard_map/mij,mjk->mik/dot_general | solution.py:28
  312.8 3.4 copy-done.2
  316.2 8.5 %fusion.10 = f32[8,128,128]{2,1,0:T(8,128)} fusion(f32[8,128,2048]{2,1,0:T(8,128)S(1)} %multiply_add_fusion.2), kind=kOutput, calls=%fused_computation.25 | convolution fusion | flops 3221225472 | bytes 8912896 | tf_op jit(solution)/shard_map/mik,mjk->mij/dot_general | solution.py:20
  324.8 21.4 %all-gather.13.cloned.1.call-done = f32[16,128,128]{2,1,0:T(8,128)} async-done(((f32[8,128,128]{2,1,0:T(8,128)}), f32[16,128,128]{2,1,0:T(8,128)}) %all-gather.13.cloned.1.call-update) | async-done | bytes 1048592 | tf_op jit(solution)/shard_map/all_gather | solution.py:19
  348.2 14.1 %multiply_add_fusion.1 = f32[8,128,2048]{2,1,0:T(8,128)S(1)} fusion(f32[8,128,2048]{2,1,0:T(8,128)} %copy-done.2, f32[8,128,128]{2,1,0:T(8,128)S(1)} %fusion.6), kind=kOutput, calls=%fused_computation.5 | convolution fusion | flops 3225419776 | bytes 17301504 | tf_op jit(solution)/shard_map/mij,mjk->mik/dot_general | solution.py:28
  362.4 3.4 copy-done.3
  365.8 8.5 %fusion.11 = f32[8,128,128]{2,1,0:T(8,128)} fusion(f32[8,128,2048]{2,1,0:T(8,128)S(1)} %multiply_add_fusion.1), kind=kOutput, calls=%fused_computation.26 | convolution fusion | flops 3221225472 | bytes 8912896 | tf_op jit(solution)/shard_map/mik,mjk->mij/dot_general | solution.py:20
  374.3 21.4 %all-gather.15.cloned.1.call-done = f32[16,128,128]{2,1,0:T(8,128)} async-done(((f32[8,128,128]{2,1,0:T(8,128)}), f32[16,128,128]{2,1,0:T(8,128)}) %all-gather.15.cloned.1.call-update) | async-done | bytes 1048592 | tf_op jit(solution)/shard_map/all_gather | solution.py:19
  397.8 14.9 %multiply_add_fusion = f32[8,128,2048]{2,1,0:T(8,128)S(1)} fusion(f32[8,128,2048]{2,1,0:T(8,128)} %copy-done.3, f32[8,128,128]{2,1,0:T(8,128)S(1)} %fusion.5), kind=kOutput, calls=%fused_computation.4 | convolution fusion | flops 3225419776 | bytes 17301504 | tf_op jit(solution)/shard_map/mij,mjk->mik/dot_general | solution.py:28
  412.6 4.9 copy.8
  417.5 188.9 %all_to_all.28 = f32[8,128,2048]{2,0,1:T(8,128)S(1)} all-to-all(f32[8,128,2048]{2,0,1:T(8,128)S(1)} %copy.8), channel_id=1, replica_groups=mesh['shard'=16,'model'=2] {'shard'}, dimensions={1} | all-to-all | bytes 16777216 | tf_op jit(solution)/shard_map/all_to_all | solution.py:31
  606.5 1.8 broadcast_multiply_fusion
  608.3 9.7 %copy.9 = f32[16,8,8,2048]{3,2,1,0:T(8,128)} copy(f32[16,8,8,2048]{3,1,2,0:T(8,128)S(1)} %bitcast.50) | data formatting | bytes 16777216 | tf_op jit(solution)/shard_map/mul | solution.py:32
  618.0 11.9 %bitcast_subtract_fusion = f32[128,8,2048]{2,1,0:T(8,128)} fusion(f32[128,8,2048]{2,1,0:T(8,128)} %param.5, f32[16,8,8,2048]{3,2,1,0:T(8,128)} %copy.9), kind=kLoop, calls=%fused_computation.1 | loop fusion | flops 2097152 | bytes 25165824 | tf_op jit(solution)/shard_map/sub | solution.py:32
  (22 shorter events, 9.0 us)
Async XLA Ops:
  7.2 242.2 %all-gather.9.cloned.1.call-start = ((), (), s32[]{:S(2)}) async-start(), calls=%async_computation.2 | async-start | bytes 1572864 | tf_op jit(solution)/shard_map/all_gather | solution.py:19
  206.2 3.4 copy-start
  227.3 69.1 %all-gather.11.cloned.1.call-start = ((), (), s32[]{:S(2)}) async-start(), calls=%async_computation.3 | async-start | bytes 1572864 | tf_op jit(solution)/shard_map/all_gather | solution.py:19
  263.1 3.4 copy-start.1
  275.0 71.2 %all-gather.13.cloned.1.call-start = ((), (), s32[]{:S(2)}) async-start(), calls=%async_computation.4 | async-start | bytes 1572864 | tf_op jit(solution)/shard_map/all_gather | solution.py:19
  312.8 3.4 copy-start.2
  324.8 71.0 %all-gather.15.cloned.1.call-start = ((), (), s32[]{:S(2)}) async-start(), calls=%async_computation.5 | async-start | bytes 1572864 | tf_op jit(solution)/shard_map/all_gather | solution.py:19
  362.4 3.4 copy-start.3
Sparse Core Ops, SparseCore 0:
  227.5 21.8 all-gather.8
  275.1 21.2 all-gather.10
  324.9 21.2 all-gather.12
  374.4 21.2 all-gather.14
